TPU v7x, 512 devices: a whole 4x8x8 slice. The times are simulated.
512 devices in a mesh: fsdp: 64 (over y, x, core), tp: 8 (over z).
Axes of the slice: x: 4, y: 8, z: 8, core: 2. Of those that a mesh axis runs over, the one named last changes fastest.
Arguments:
- grads: bfloat16 [128, 128, 8192], P('tp', None, 'fsdp'), may hold values from -60 to 60
- momentum: bfloat16 [128, 128, 8192], P('tp', None, 'fsdp'), may hold values from -6 to 6
- owner_table: int32 [128, 1], P('tp'), may hold values from 0 to 63; in each aligned block of 16 rows (0 to 15, 16 to 31, ...) at most 2 rows name the same one
- pool_map: int32 [8, 16], P('tp'), may hold values from 0 to 15, each once within a row
Outputs:
- new_momentum: bfloat16 [128, 128, 8192], P('tp', None, 'fsdp')
- pool_update: bfloat16 [128, 128, 8192], P('tp', None, 'fsdp')
- slot_rms: float32 [8, 128], P('tp', 'fsdp')
Inputs may be any that keep to these rules, and one draw needn't show every extreme that they name: `owner_table`: within each aligned block of 16 rows (the head blocks of one index of tp) no owner is named more than 2 times. `pool_map`: each row is a permutation of 0 to 15.
All inputs are finite; a program needn't handle non-finite values.
Results may differ from a plain program's by a relative error of at most 0.0058.
Values may be sent and summed in bfloat16 or wider, within the bound.
A program may use at most 64 MiB of HBM per device.

v0:
```python
import math

import jax
import jax.numpy as jnp
from jax import lax
from jax.sharding import PartitionSpec as P

D = 8192
CAP = 2
ITERS = 3


momentum_rate = 0.95
step_size = 0.8
epsilon = 1e-07
poly_linear = 3.4445
poly_cubic = -4.775
poly_quintic = 2.0315


def in_blocks(x, dim, size):
    before, after = (x.shape[:dim], x.shape[dim + 1 :])
    return jnp.moveaxis(x.reshape(*before, size, -1, *after), dim, 0)


def cut_rows(length, count):
    lap = length // count
    if lap >= 8:
        lap -= lap % 8
    return [lap * k for k in range(1, count)]


def joined_along(pieces, dim):
    pieces = jnp.moveaxis(pieces, 0, dim)
    lengths = pieces.shape
    return pieces.reshape(*lengths[:dim], lengths[dim] * lengths[dim + 1], *lengths[dim + 2 :])


def exchange_in_pieces(x, axis, pieces, split_dim, concat_dim):
    blocks = in_blocks(x, split_dim, lax.axis_size(axis))
    cut = max(range(1, max(2, blocks.ndim - 1)), key=lambda d: blocks.shape[d])
    outs = []
    for share in jnp.split(blocks, cut_rows(blocks.shape[cut], pieces), axis=cut):
        if share.size:
            outs.append(lax.all_to_all(share, axis, split_axis=0, concat_axis=0, tiled=True))
    return joined_along(jnp.concatenate(outs, axis=cut), concat_dim)


def sent_to_all(x, axis):
    size = lax.axis_size(axis)
    return lax.all_to_all(jnp.broadcast_to(x[None], (size, *x.shape)), axis, 0, 0, tiled=True)


def gathered_copies(x, axis, dim):
    pieces = sent_to_all(x, axis)
    return joined_along(pieces, dim)


def orthogonalize(arrived):
    values = arrived[:, 0].astype(jnp.float32)
    squares = jnp.sum(values * values, axis=(1, 2))
    inverse = 1.0 / (jnp.sqrt(squares) + epsilon)
    gram = (
        jnp.einsum("kij,klj->kil", values, values, precision=lax.Precision.HIGHEST)
        * (inverse * inverse)[:, None, None]
    )
    identity = jnp.eye(values.shape[1], dtype=jnp.float32)[None]
    transform = identity
    for _ in range(ITERS):
        square_gram = jnp.einsum("kil,klm->kim", gram, gram, precision=lax.Precision.HIGHEST)
        mixed = poly_linear * identity + poly_cubic * gram + poly_quintic * square_gram
        transform = jnp.einsum("kil,klm->kim", mixed, transform, precision=lax.Precision.HIGHEST)
        right_side = jnp.einsum("kil,klm->kim", gram, mixed, precision=lax.Precision.HIGHEST)
        gram = jnp.einsum("kil,klm->kim", mixed, right_side, precision=lax.Precision.HIGHEST)
    scaled = transform * inverse[:, None, None]
    current = jnp.einsum("kil,klj->kij", scaled, values, precision=lax.Precision.HIGHEST)
    rms_values = jnp.sqrt(squares / (values.shape[1] * values.shape[2]))
    return (current.astype(jnp.bfloat16)[:, None], rms_values)


def worker_work(arrived):
    ortho, rms_values = orthogonalize(arrived)
    returned = exchange_in_pieces(ortho, "fsdp", 2, 3, 1)
    return (returned, rms_values)


def local(grads, momentum, owner_table, pool_map):
    devices_fsdp = lax.axis_size("fsdp")
    blocks = grads.shape[0]
    velocity = momentum_rate * momentum.astype(jnp.float32) + grads.astype(jnp.float32)
    new_momentum = velocity.astype(jnp.bfloat16)
    nesterov = (grads.astype(jnp.float32) + momentum_rate * velocity).astype(jnp.bfloat16)
    owners = owner_table[:, 0]
    position = jnp.arange(blocks, dtype=jnp.int32)
    earlier = position[None, :] < position[:, None]
    same_owner = owners[:, None] == owners[None, :]
    slots = jnp.sum(jnp.logical_and(same_owner, earlier), axis=1)
    slot_range = jnp.arange(CAP, dtype=jnp.int32)
    spread = -(-blocks // devices_fsdp)
    padded = jnp.pad(nesterov, ((0, spread * devices_fsdp - blocks), (0, 0), (0, 0)))
    packed = padded.reshape(spread, devices_fsdp, grads.shape[1], grads.shape[2])
    returned, rms_values = worker_work(
        lax.all_to_all(packed, "fsdp", split_axis=1, concat_axis=3, tiled=True)
    )
    ortho_local = returned.reshape(spread * devices_fsdp, grads.shape[1], grads.shape[2])[:blocks]
    gathered = gathered_copies(rms_values, "fsdp", 0)
    by_block = gathered.reshape(devices_fsdp, spread).T.reshape(-1)[:blocks]
    here = lax.axis_index("fsdp")
    pick = jnp.logical_and((owners == here)[None, :], slots[None, :] == slot_range[:, None]).astype(
        jnp.float32
    )
    slot_out = jnp.dot(pick, by_block, precision=lax.Precision.HIGHEST)[None, :]
    factor = step_size * 0.2 * math.sqrt(D)
    update = (-factor * ortho_local.astype(jnp.float32)).astype(jnp.bfloat16)
    codes = pool_map[0]
    permute = (codes[None, :] == position[:, None]).astype(jnp.bfloat16)
    ordered = jnp.einsum("qb,bhs->qhs", permute, update, preferred_element_type=jnp.float32).astype(
        jnp.bfloat16
    )
    pool_update = lax.all_to_all(ordered, "tp", split_axis=0, concat_axis=0, tiled=True)
    return (new_momentum, pool_update, slot_out)


def solution(mesh):
    in_specs = (P("tp", None, "fsdp"), P("tp", None, "fsdp"), P("tp", None), P("tp", None))
    out_specs = (P("tp", None, "fsdp"), P("tp", None, "fsdp"), P("tp", "fsdp"))
    return jax.shard_map(local, mesh=mesh, in_specs=in_specs, out_specs=out_specs, check_vma=False)
```

profile of v0, /device:TPU:1, one launch (start us, length us, event | category | flops | bytes accessed | tf_op | source)
XLA Modules:
  0.0 193.6 jit_solution(3435706301445865622)
XLA Ops:
  0.6 2.3 %fusion.12 = (bf16[16,128,128]{2,1,0:T(8,128)(2,1)S(1)}, bf16[16,128,128]{2,1,0:T(8,128)(2,1)}) fusion(bf16[16,128,128]{2,1,0:T(8,128)(2,1)} %param.4, bf16[16,128,128]{2,1,0:T(8,128)(2,1)} %param.5), kind=kLoop, calls=%fused_computation.19 | loop fusion | flops 2097152 | bytes 2097152 | tf_op jit(solution)/shard_map/convert_element_type | solution.py:92
  2.9 0.4 pad_bitcast_fusion
  3.3 61.1 %all_to_all.36 = bf16[1,64,128,128]{3,2,0,1:T(8,128)(2,1)S(1)} all-to-all(bf16[1,64,128,128]{3,2,0,1:T(8,128)(2,1)S(1)} %pad_bitcast_fusion), channel_id=1, replica_groups=mesh['fsdp'=64,'tp'=8] {'fsdp'}, dimensions={1} | all-to-all | bytes 4194304 | tf_op jit(solution)/shard_map/all_to_all | solution.py:103
  64.4 1.7 multiply_reduce_fusion
  66.8 0.7 fusion.9
  67.6 0.2 fusion.8
  67.8 0.2 fusion.31
  68.2 0.2 fusion.32
  68.4 0.2 fusion.7
  68.6 0.2 fusion.33
  68.8 0.2 fusion.35
  69.0 0.2 fusion.34
  69.2 0.2 fusion.6
  69.4 2.9 %copy.20 = bf16[1,1,128,64,128]{2,4,3,1,0:T(8,128)(2,1)} copy(bf16[1,1,128,64,128]{4,2,3,1,0:T(8,128)(2,1)S(1)} %bitcast.60) | data formatting | bytes 4194304 | tf_op jit(solution)/shard_map/all_to_all | solution.py:103
  72.6 3.4 %fusion.2 = bf16[16,8,64,128]{3,1,2,0:T(8,128)(2,1)S(1)} fusion(f32[128,128]{1,0:T(8,128)S(1)} %convolution_multiply_fusion, bf16[128,8192]{0,1:T(8,128)(2,1)} %bitcast.61), kind=kOutput, calls=%fused_computation.6 | convolution fusion | flops 1611661312 | bytes 4259840 | tf_op jit(solution)/shard_map/kil,klj->kij/dot_general | solution.py:76
  76.0 0.6 copy.25
  76.6 1.4 copy.27
  77.9 1.1 fusion.30
  79.1 34.9 %all_to_all.37 = bf16[64,1,1,64,128]{4,3,2,1,0:T(8,128)(2,1)S(1)} all-to-all(bf16[64,1,1,64,128]{4,3,2,1,0:T(8,128)(2,1)S(1)} %get-tuple-element.9), channel_id=1, replica_groups=mesh['fsdp'=64,'tp'=8] {'fsdp'}, dimensions={0} | all-to-all | bytes 2097152 | tf_op jit(solution)/shard_map/all_to_all | solution.py:45
  114.0 6.3 %all-to-all-start.2 = ((bf16[64,1,1,64,128]{4,3,2,1,0:T(8,128)(2,1)}), bf16[64,1,1,64,128]{4,3,2,1,0:T(8,128)(2,1)S(1)}, u32[]{:S(2)}, u32[]{:S(2)}) async-start(bf16[64,1,1,64,128]{4,3,2,1,0:T(8,128)(2,1)} %get-tuple-element.10), calls=%async_computation.2 | async-start | bytes 2097152 | tf_op jit(solution)/shard_map/all_to_all | solution.py:45
  121.0 0.7 copy.22
  121.7 26.8 %all-to-all-done.2 = bf16[64,1,1,64,128]{4,3,2,1,0:T(8,128)(2,1)S(1)} async-done(((bf16[64,1,1,64,128]{4,3,2,1,0:T(8,128)(2,1)}), bf16[64,1,1,64,128]{4,3,2,1,0:T(8,128)(2,1)S(1)}, u32[]{:S(2)}, u32[]{:S(2)}) %all-to-all-start.2) | async-done | bytes 1048608 | tf_op jit(solution)/shard_map/all_to_all | solution.py:45
  148.5 0.6 broadcast_in_dim.4
  149.1 6.3 %all-to-all-start.4 = ((f32[64,1,1]{2,1,0:T(1,128)}), f32[64,1,1]{2,1,0:T(1,128)S(1)}, u32[]{:S(2)}, u32[]{:S(2)}) async-start(f32[64,1,1]{2,1,0:T(1,128)} %broadcast_in_dim.4), calls=%async_computation.4 | async-start | bytes 65536 | tf_op jit(solution)/shard_map/all_to_all | solution.py:51
  155.4 0.7 copy.23
  156.1 0.3 convolution_convert_fusion.1
  156.4 0.9 copy.24
  157.3 7.5 %all-to-all-done.4 = f32[64,1,1]{2,1,0:T(1,128)S(1)} async-done(((f32[64,1,1]{2,1,0:T(1,128)}), f32[64,1,1]{2,1,0:T(1,128)S(1)}, u32[]{:S(2)}, u32[]{:S(2)}) %all-to-all-start.4) | async-done | bytes 288 | tf_op jit(solution)/shard_map/all_to_all | solution.py:51
  164.8 10.0 %all-to-all-start.3 = ((bf16[16,128,128]{2,1,0:T(8,128)(2,1)}), bf16[16,128,128]{2,1,0:T(8,128)(2,1)S(1)}, u32[]{:S(2)}, u32[]{:S(2)}) async-start(bf16[16,128,128]{2,1,0:T(8,128)(2,1)} %copy.24), calls=%async_computation.3 | async-start | bytes 1048576 | tf_op jit(solution)/shard_map/all_to_all | solution.py:120
  175.2 0.6 fusion.23
  175.9 16.9 %all-to-all-done.3 = bf16[16,128,128]{2,1,0:T(8,128)(2,1)S(1)} async-done(((bf16[16,128,128]{2,1,0:T(8,128)(2,1)}), bf16[16,128,128]{2,1,0:T(8,128)(2,1)S(1)}, u32[]{:S(2)}, u32[]{:S(2)}) %all-to-all-start.3) | async-done | bytes 524320 | tf_op jit(solution)/shard_map/all_to_all | solution.py:120
  192.8 0.8 copy.29
  (9 shorter events, 0.8 us)
Async XLA Ops:
  114.0 34.4 %all-to-all-start.2 = ((bf16[64,1,1,64,128]{4,3,2,1,0:T(8,128)(2,1)}), bf16[64,1,1,64,128]{4,3,2,1,0:T(8,128)(2,1)S(1)}, u32[]{:S(2)}, u32[]{:S(2)}) async-start(bf16[64,1,1,64,128]{4,3,2,1,0:T(8,128)(2,1)} %get-tuple-element.10), calls=%async_computation.2 | async-start | bytes 2097152 | tf_op jit(solution)/shard_map/all_to_all | solution.py:45
  121.0 35.1 %copy-start = (s32[1,16]{1,0:T(1,128)S(1)}, s32[1,16]{1,0:T(1,128)}, u32[]{:S(2)}) copy-start(s32[1,16]{1,0:T(1,128)} %param.7) | copy-start | bytes 196
  149.1 15.7 %all-to-all-start.4 = ((f32[64,1,1]{2,1,0:T(1,128)}), f32[64,1,1]{2,1,0:T(1,128)S(1)}, u32[]{:S(2)}, u32[]{:S(2)}) async-start(f32[64,1,1]{2,1,0:T(1,128)} %broadcast_in_dim.4), calls=%async_computation.4 | async-start | bytes 65536 | tf_op jit(solution)/shard_map/all_to_all | solution.py:51
  156.1 18.8 %copy-start.1 = (s32[16,1]{0,1:T(1,128)S(1)}, s32[16,1]{0,1:T(1,128)}, u32[]{:S(2)}) copy-start(s32[16,1]{0,1:T(1,128)} %param.6) | copy-start | bytes 196
  164.8 28.0 %all-to-all-start.3 = ((bf16[16,128,128]{2,1,0:T(8,128)(2,1)}), bf16[16,128,128]{2,1,0:T(8,128)(2,1)S(1)}, u32[]{:S(2)}, u32[]{:S(2)}) async-start(bf16[16,128,128]{2,1,0:T(8,128)(2,1)} %copy.24), calls=%async_computation.3 | async-start | bytes 1048576 | tf_op jit(solution)/shard_map/all_to_all | solution.py:120
where the time goes:
time: 194 us
  blocking collectives  96 us (49%)
  waiting for transfers between devices  51.2 us (26%)
  starting transfers between devices  22.6 us (12%)
  local copies, waits for them, and re-layouts  10.4 us (5%)
  matrix products  7.03 us (4%)
  other arithmetic  4.13 us (2%)
  between operations  2.25 us (1%)
    all_to_all x1, blocking collectives, local(): lax.all_to_all(packed, 'fsdp', split_axis=1, concat_axis=3, tiled=True)  61.1 us
    all_to_all x1, blocking collectives, exchange_in_pieces(): lax.all_to_all(share, axis, split_axis=0, concat_axis=0, tiled=True)  34.9 us
    all_to_all x1, waiting for transfers between devices, exchange_in_pieces(): lax.all_to_all(share, axis, split_axis=0, concat_axis=0, tiled=True)  26.8 us
    all_to_all x1, waiting for transfers between devices, local(): lax.all_to_all(ordered, 'tp', split_axis=0, concat_axis=0, tiled=True)  16.9 us
    all_to_all x1, starting transfers between devices, local(): lax.all_to_all(ordered, 'tp', split_axis=0, concat_axis=0, tiled=True)  10 us
    all_to_all x1, waiting for transfers between devices, sent_to_all(): lax.all_to_all(jnp.broadcast_to(x[None], (size, *x.shape)), axis, 0, 0, t...  7.48 us
    all_to_all x1, starting transfers between devices, exchange_in_pieces(): lax.all_to_all(share, axis, split_axis=0, concat_axis=0, tiled=True)  6.27 us
    all_to_all x1, starting transfers between devices, sent_to_all(): lax.all_to_all(jnp.broadcast_to(x[None], (size, *x.shape)), axis, 0, 0, t...  6.27 us
  transfers between devices with their start and end apart: 3, of which 3 were waited for; matrix products, arithmetic and copies ran while one was open for 2% of the time, Pallas kernels for 0%

commit v1 on v0

v1 whole, which is shorter than its diff:
```python
import functools
import math

import jax
import jax.numpy as jnp
from jax import lax
from jax.experimental import pallas as pl
from jax.experimental.pallas import tpu as pltpu
from jax.sharding import PartitionSpec as P

ITERS = 3
momentum_rate = 0.95
step_size = 0.8
epsilon = 1e-07
poly_linear = 3.4445
poly_cubic = -4.775
poly_quintic = 2.0315

H = 128
PACKED = H + 8
MESH = pl.DeviceIdType.MESH


def masks():
    row = lax.broadcasted_iota(jnp.int32, (H, H), 0)
    col = lax.broadcasted_iota(jnp.int32, (H, H), 1)
    return row >= col, row == col


def put_packed(ref, a, b):
    low, diag = masks()
    ref[0:H, :] = jnp.where(low, a, b)
    last = jnp.sum(jnp.where(diag, b, 0.0), axis=0, keepdims=True)
    ref[H:PACKED, :] = jnp.broadcast_to(last, (8, H))


def get_packed(ref):
    low, diag = masks()
    both = ref[0:H, :]
    other = both.T
    last = jnp.broadcast_to(ref[H : H + 1, :], (H, H))
    a = jnp.where(low, both, other)
    b = jnp.where(diag, last, jnp.where(low, other, both))
    return a, b


def dot32(a, b):
    return jnp.dot(a, b, precision=lax.Precision.HIGHEST, preferred_element_type=jnp.float32)


def newton_schulz(grams):
    _, diag = masks()
    identity = jnp.where(diag, 1.0, 0.0)
    inverses, gs, qs = [], [], [None] * len(grams)
    for g in grams:
        squares = jnp.sum(jnp.where(diag, g, 0.0), keepdims=True)
        inverse = 1.0 / (jnp.sqrt(squares) + epsilon)
        inverses.append(inverse)
        gs.append(g * (inverse * inverse))
    for it in range(ITERS):
        g2 = [dot32(g, g) for g in gs]
        ms = [poly_linear * identity + poly_cubic * g + poly_quintic * s for g, s in zip(gs, g2)]
        if it < ITERS - 1:
            right = [dot32(g, m) for g, m in zip(gs, ms)]
        qs = [m if it == 0 else dot32(m, q) for m, q in zip(ms, qs)]
        if it < ITERS - 1:
            gs = [dot32(m, r) for m, r in zip(ms, right)]
    return [q * inverse for q, inverse in zip(qs, inverses)]


def kernel(
    sizes,
    owner_ref,
    pool_ref,
    g_hbm,
    m_hbm,
    nm_hbm,
    out_hbm,
    slot_ref,
    gbuf,
    mbuf,
    nmbuf,
    nes,
    yq,
    yr,
    pk,
    r0,
    s1,
    r1,
    s2,
    r2,
    rd,
    s3,
    sd,
    gram,
    qall,
    outbuf,
    t0,
    t0r,
    t1,
    t1r,
    t2,
    t2r,
    in_sem,
    nm_sem,
    out_sem,
    z_send,
    z_recv,
    c_send,
    c_recv,
    x_send,
    x_recv,
    y_send,
    y_recv,
    t_send,
    t_recv,
    w_send,
    w_recv,
    a_send,
    a_recv,
    b_send,
    b_recv,
):
    NX, NY, NZ, NB = sizes
    NK = 2 * NX
    CH = H // NY
    f = lax.axis_index("fsdp")
    z = lax.axis_index("tp")
    k = lax.rem(f, NK)
    y = lax.div(f, NK)
    x = lax.div(k, 2)
    c = lax.rem(k, 2)

    def dev(yy, xx, cc, zz):
        return ((yy * NX + xx) * 2 + cc, zz)

    partner = dev(y, x, 1 - c, z)

    def xdev(d):
        return dev(y, lax.rem(x + d, NX), c, z)

    def ydev(d):
        return dev(lax.rem(y + d, NY), x, c, z)

    def zdev(d):
        return dev(y, x, c, lax.rem(z + d, NZ))

    def wdev(d):
        return (lax.rem(y + d, NY) * NK + z, k)

    def remote(src, dst, send, recv, device):
        return pltpu.make_async_remote_copy(
            src_ref=src, dst_ref=dst, send_sem=send, recv_sem=recv, device_id=device, device_id_type=MESH
        )

    CHUNKS = 4
    per = NB // CHUNKS
    loads = []
    for i in range(CHUNKS):
        part = pl.ds(i * per, per)
        lg = pltpu.make_async_copy(g_hbm.at[part], gbuf.at[part], in_sem.at[2 * i])
        lm = pltpu.make_async_copy(m_hbm.at[part], mbuf.at[part], in_sem.at[2 * i + 1])
        lg.start()
        lm.start()
        loads.append((lg, lm))

    barrier = pltpu.get_barrier_semaphore()

    def greet(device):
        pl.semaphore_signal(barrier, inc=1, device_id=device, device_id_type=MESH)

    for d in range(1, NZ):
        greet(zdev(d))
    for d in range(1, NY):
        greet(ydev(d))
    for d in range(1, NX):
        greet(xdev(d))
    greet(partner)

    @pl.when(k != z)
    def _():
        for d in range(NY):
            greet(wdev(d))

    codes = [pool_ref[0, j] for j in range(NB)]
    source = []
    for q in range(NB):
        at = jnp.int32(0)
        for j in range(1, NB):
            at = jnp.where(codes[j] == q, j, at)
        source.append(at)

    stores = []
    for i in range(CHUNKS):
        for cp in loads[i]:
            cp.wait()
        for j in range(i * per, (i + 1) * per):
            grad = gbuf[j].astype(jnp.float32)
            velocity = momentum_rate * mbuf[j].astype(jnp.float32) + grad
            nmbuf[j] = velocity.astype(jnp.bfloat16)
            nes[j] = (grad + momentum_rate * velocity).astype(jnp.bfloat16)
        part = pl.ds(i * per, per)
        st = pltpu.make_async_copy(nmbuf.at[part], nm_hbm.at[part], nm_sem.at[i])
        st.start()
        stores.append(st)

    for p in range(NZ):
        grams = []
        for e in range(2):
            q = 2 * p + e
            value = nes[source[q]]
            yq[q] = value
            wide = value.astype(jnp.float32)
            t0[q : q + 1, :] = jnp.sum(wide * wide, axis=0, keepdims=True)
            grams.append(
                lax.dot_general(value, value, (((1,), (1,)), ((), ())), preferred_element_type=jnp.float32)
            )
        put_packed(pk.at[p % 2, p // 2], *grams)

    pl.semaphore_wait(barrier, (NZ - 1) + (NY - 1) + (NX - 1) + 1 + jnp.where(k != z, NY, 0))

    sent = []

    def go(copy):
        copy.start()
        sent.append(copy)
        return copy

    cc = go(remote(pk.at[1 - c], r0, c_send.at[0], c_recv.at[0], partner))
    ct = go(remote(t0, t0r, c_send.at[1], c_recv.at[1], partner))
    zc = []
    for d in sorted(range(1, NZ), key=lambda d: -min(d, NZ - d)):
        to = lax.rem(z + d, NZ)
        zc.append(go(remote(yq.at[pl.ds(2 * to, 2)], yr.at[pl.ds(2 * z, 2)], z_send.at[d], z_recv.at[d], zdev(d))))
    mine = pltpu.make_async_copy(yq.at[pl.ds(2 * z, 2)], yr.at[pl.ds(2 * z, 2)], z_recv.at[0])
    mine.start()

    cc.wait_recv()
    for i in range(NX):
        s1[i] = pk[c, i] + r0[i]
    xc = []
    for d in range(1, NX):
        to = lax.rem(x + d, NX)
        xc.append(go(remote(s1.at[to], r1.at[d - 1], x_send.at[d], x_recv.at[d], xdev(d))))
    ct.wait_recv()
    t1[...] = t0[...] + t0r[...]
    tx = [go(remote(t1, t1r.at[d - 1], t_send.at[d], t_recv.at[d], xdev(d))) for d in range(1, NX)]

    for cp in xc:
        cp.wait_recv()
    total = s1[x]
    for d in range(1, NX):
        total = total + r1[d - 1]
    s2[...] = total
    yc, yd = [], []
    for d in sorted(range(1, NY), key=lambda d: -min(d, NY - d)):
        to = lax.rem(y + d, NY)
        rows = pl.ds(pl.multiple_of(to * CH, CH), CH)
        yc.append(go(remote(s2.at[rows], r2.at[d - 1], y_send.at[d], y_recv.at[d], ydev(d))))
    for d in range(1, NY):
        yd.append(go(remote(s2.at[pl.ds(H, 8)], rd.at[d - 1], y_send.at[NY + d], y_recv.at[NY + d], ydev(d))))
    for cp in tx:
        cp.wait_recv()
    ttotal = t1[...]
    for d in range(1, NX):
        ttotal = ttotal + t1r[d - 1]
    t2[...] = ttotal
    ty = [go(remote(t2, t2r.at[d - 1], t_send.at[NX + d], t_recv.at[NX + d], ydev(d))) for d in range(1, NY)]

    for cp in yc:
        cp.wait_recv()
    total = s2[pl.ds(pl.multiple_of(y * CH, CH), CH), :]
    for d in range(1, NY):
        total = total + r2[d - 1]
    s3[...] = total
    own_rows = pl.ds(pl.multiple_of(y * CH, CH), CH)
    wc = []
    for d in sorted(range(1, NY), key=lambda d: -min(d, NY - d)):
        wc.append(go(remote(s3, gram.at[own_rows], w_send.at[d], w_recv.at[d], wdev(d))))
    for cp in yd:
        cp.wait_recv()
    total = s2[pl.ds(H, 8), :]
    for d in range(1, NY):
        total = total + rd[d - 1]
    sd[...] = total
    w0 = remote(s3, gram.at[own_rows], w_send.at[0], w_recv.at[0], wdev(0))
    w1 = remote(sd, gram.at[pl.ds(H, 8)], w_send.at[NY], w_recv.at[NY], wdev(0))
    l0 = pltpu.make_async_copy(s3, gram.at[own_rows], w_recv.at[0])
    l1 = pltpu.make_async_copy(sd, gram.at[pl.ds(H, 8)], w_recv.at[NY])

    @pl.when(k != z)
    def _():
        w0.start()
        w1.start()

    @pl.when(k == z)
    def _():
        l0.start()
        l1.start()

    for cp in ty:
        cp.wait_recv()
    ttotal = t2[...]
    for d in range(1, NY):
        ttotal = ttotal + t2r[d - 1]
    t2r[NY - 1] = ttotal
    count = jnp.int32(0)
    picked = [jnp.zeros((1, H), jnp.float32), jnp.zeros((1, H), jnp.float32)]
    for j in range(NB):
        same = jnp.where(owner_ref[0, j] == f, 1, 0)
        line = t2r[NY - 1, pl.ds(codes[j], 1), :]
        for s in range(2):
            weight = jnp.where(count == s, same, 0).astype(jnp.float32)
            picked[s] = picked[s] + line * weight
        count = count + same
    lane = lax.broadcasted_iota(jnp.int32, (1, 2), 1)
    sums = [jnp.sum(v, axis=1, keepdims=True) for v in picked]
    elements = H * H * NK * NY
    slot_ref[...] = jnp.sqrt(jnp.where(lane == 0, sums[0], sums[1]) / elements)

    for cp in wc:
        cp.wait_recv()
    l0.wait()
    l1.wait()
    a, b = newton_schulz(list(get_packed(gram)))
    put_packed(qall.at[k], a, b)

    xa = []
    b_own = go(remote(qall.at[k], qall.at[k], b_send.at[0], b_recv.at[0], partner))
    for d in range(1, NX):
        xa.append(go(remote(qall.at[k], qall.at[k], a_send.at[d], a_recv.at[d], xdev(d))))

    mine.wait()
    for cp in zc:
        cp.wait_recv()
    factor = step_size * 0.2 * math.sqrt(H * NK * NY)
    outs = []

    def apply(slot, i):
        for e, q in enumerate(get_packed(qall.at[slot])):
            high = q.astype(jnp.bfloat16)
            rest = (q - high.astype(jnp.float32)).astype(jnp.bfloat16)
            value = yr[2 * slot + e]
            ortho = jnp.dot(
                jnp.concatenate([high, rest], axis=1),
                jnp.concatenate([value, value], axis=0),
                preferred_element_type=jnp.float32,
            ).astype(jnp.bfloat16)
            outbuf[2 * slot + e] = (-factor * ortho.astype(jnp.float32)).astype(jnp.bfloat16)
        part = pl.ds(2 * slot, 2)
        st = pltpu.make_async_copy(outbuf.at[part], out_hbm.at[part], out_sem.at[i])
        st.start()
        outs.append(st)

    apply(k, 0)
    b_own.wait_recv()
    apply(2 * x + 1 - c, 1)
    fwd = []
    for d in range(1, NX):
        xa[d - 1].wait_recv()
        slot = 2 * lax.rem(x + NX - d, NX) + c
        fwd.append(go(remote(qall.at[slot], qall.at[slot], b_send.at[d], b_recv.at[d], partner)))
        apply(slot, 2 * d)
    for d in range(1, NX):
        fwd[d - 1].wait_recv()
        apply(2 * lax.rem(x + NX - d, NX) + 1 - c, 2 * d + 1)

    for st in outs + stores:
        st.wait()
    for cp in sent:
        cp.wait_send()

    @pl.when(k != z)
    def _():
        w0.wait_send()
        w1.wait_send()


def local(sizes, grads, momentum, owner_table, pool_map):
    NX, NY, NZ, NB = sizes
    NK = 2 * NX
    f32, bf16 = jnp.float32, jnp.bfloat16
    dma = pltpu.SemaphoreType.DMA
    hbm = pl.BlockSpec(memory_space=pl.ANY)
    scratch = [
        pltpu.VMEM((NB, H, H), bf16),
        pltpu.VMEM((NB, H, H), bf16),
        pltpu.VMEM((NB, H, H), bf16),
        pltpu.VMEM((NB, H, H), bf16),
        pltpu.VMEM((NB, H, H), bf16),
        pltpu.VMEM((NB, H, H), bf16),
        pltpu.VMEM((2, NX, PACKED, H), f32),
        pltpu.VMEM((NX, PACKED, H), f32),
        pltpu.VMEM((NX, PACKED, H), f32),
        pltpu.VMEM((NX - 1, PACKED, H), f32),
        pltpu.VMEM((PACKED, H), f32),
        pltpu.VMEM((NY - 1, H // NY, H), f32),
        pltpu.VMEM((NY - 1, 8, H), f32),
        pltpu.VMEM((H // NY, H), f32),
        pltpu.VMEM((8, H), f32),
        pltpu.VMEM((PACKED, H), f32),
        pltpu.VMEM((NK, PACKED, H), f32),
        pltpu.VMEM((NB, H, H), bf16),
        pltpu.VMEM((NB, H), f32),
        pltpu.VMEM((NB, H), f32),
        pltpu.VMEM((NB, H), f32),
        pltpu.VMEM((NX - 1, NB, H), f32),
        pltpu.VMEM((NB, H), f32),
        pltpu.VMEM((NY, NB, H), f32),
        dma((8,)),
        dma((4,)),
        dma((NK,)),
        dma((NZ,)),
        dma((NZ,)),
        dma((2,)),
        dma((2,)),
        dma((NX,)),
        dma((NX,)),
        dma((2 * NY,)),
        dma((2 * NY,)),
        dma((NX + NY,)),
        dma((NX + NY,)),
        dma((NY + 1,)),
        dma((NY + 1,)),
        dma((NX,)),
        dma((NX,)),
        dma((NX,)),
        dma((NX,)),
    ]
    smem = pl.BlockSpec(memory_space=pltpu.SMEM)
    return pl.pallas_call(
        functools.partial(kernel, sizes),
        out_shape=(
            jax.ShapeDtypeStruct(grads.shape, bf16),
            jax.ShapeDtypeStruct(grads.shape, bf16),
            jax.ShapeDtypeStruct((1, 2), f32),
        ),
        in_specs=[smem, smem, hbm, hbm],
        out_specs=(hbm, hbm, pl.BlockSpec(memory_space=pltpu.VMEM)),
        scratch_shapes=scratch,
        compiler_params=pltpu.CompilerParams(
            collective_id=0, has_side_effects=True
        ),
    )(owner_table.reshape(1, NB), pool_map, grads, momentum)


def solution(mesh, sizes=(4, 8, 8, 16)):
    in_specs = (P("tp", None, "fsdp"), P("tp", None, "fsdp"), P("tp", None), P("tp", None))
    out_specs = (P("tp", None, "fsdp"), P("tp", None, "fsdp"), P("tp", "fsdp"))
    return jax.shard_map(
        functools.partial(local, sizes), mesh=mesh, in_specs=in_specs, out_specs=out_specs, check_vma=False
    )
```

time: 194 us -> 52.8 us (0.27)
  blocking collectives: 96 us -> 0 us
  waiting for transfers between devices: 51.2 us -> 0 us
  Pallas kernels: 0 us -> 48.8 us
  starting transfers between devices: 22.6 us -> 0 us
  local copies, waits for them, and re-layouts: 10.4 us -> 3.25 us
  matrix products: 7.03 us -> 0 us
  other arithmetic: 4.13 us -> 0 us
    all_to_all x2 -> x0, blocking collectives: 96 us -> none  [the longest x1 61.1 us: local(): lax.all_to_all(packed, 'fsdp', split_axis=1, concat_axis=3, tiled=True)]
    all_to_all x3 -> x0, waiting for transfers between devices: 51.2 us -> none  [the longest x1 26.8 us: exchange_in_pieces(): lax.all_to_all(share, axis, split_axis=0, concat_axis=0, tiled=True)]
    pallas_call x0 -> x1, Pallas kernels: none -> 48.8 us  [local(): pl.pallas_call(functools.partial(kernel, sizes), out_shape=(jax.ShapeDtyp...]
    all_to_all x3 -> x0, starting transfers between devices: 22.6 us -> none  [the longest x1 10 us: local(): lax.all_to_all(ordered, 'tp', split_axis=0, concat_axis=0, tiled=True)]
    dot_general x14 -> x0, matrix products: 7.03 us -> none  [the longest x1 3.39 us: orthogonalize(): jnp.einsum('kil,klj->kij', scaled, values, precision=lax.Precision.HIGHEST)]
    all_to_all x3 -> x0, local copies, waits for them, and re-layouts: 4.28 us -> none  [the longest x1 2.92 us: local(): lax.all_to_all(packed, 'fsdp', split_axis=1, concat_axis=3, tiled=True)]
    convert_element_type x1 -> x0, other arithmetic: 2.27 us -> none  [local(): (grads.astype(jnp.float32) + momentum_rate * velocity).astype(jnp.bfloat16)]
  transfers between devices with their start and end apart: 3 -> 0, of which waited for: 3 -> 0; matrix products, arithmetic and copies ran while one was open for 2% -> 0% of each run, Pallas kernels for 0% -> 0%
where the time goes in v1:
time: 52.8 us; the launch traced here: 52.7 us
  Pallas kernels  48.8 us (92%)
  local copies, waits for them, and re-layouts  3.25 us (6%)
  between operations  0.65 us (1%)
    pallas_call x1, Pallas kernels, local(): pl.pallas_call(functools.partial(kernel, sizes), out_shape=(jax.ShapeDtyp...  48.8 us
    unnamed x7, local copies, waits for them, and re-layouts  3.25 us

profile of v1, /device:TPU:1, one launch (start us, length us, event | category | flops | bytes accessed | tf_op | source)
XLA Modules:
  0.0 52.7 jit_solution(9724981305975967475)
XLA Ops:
  0.6 48.8 %shard_map.67 = (bf16[16,128,128]{2,1,0:T(8,128)(2,1)}, bf16[16,128,128]{2,1,0:T(8,128)(2,1)}, f32[1,2]{1,0:T(1,128)}) custom-call(s32[1,16]{1,0:T(1,128)} %bitcast.1, s32[1,16]{1,0:T(1,128)} %pool_ref.1, bf16[16,128,128]{2,1,0:T(8,128)(2,1)} %g_hbm.1, bf16[16,128,128]{2,1,0:T(8,128)(2,1)} %m_hbm.1), custom_call_target="tpu_custom_call" | custom-call | tf_op jit(solution)/shard_map/pallas_call | solution.py:431
  49.4 0.0 copy-start
  49.4 1.9 %copy.10 = bf16[16,128,128]{2,1,0:T(8,128)(2,1)} copy(bf16[16,128,128]{2,1,0:T(8,128)(2,1)} %get-tuple-element.6) | data formatting | bytes 1048576
  51.4 0.0 copy-done
  51.4 0.0 copy-start.1
  51.4 0.8 %copy.11 = bf16[16,128,128]{2,1,0:T(8,128)(2,1)} copy(bf16[16,128,128]{2,1,0:T(8,128)(2,1)S(1)} %copy-done) | data formatting | bytes 1048576
  52.2 0.0 copy-done.1
  52.2 0.5 copy.12
Async XLA Ops:
  49.4 2.0 %copy-start = (bf16[16,128,128]{2,1,0:T(8,128)(2,1)S(1)}, bf16[16,128,128]{2,1,0:T(8,128)(2,1)}, u32[]{:S(2)}) copy-start(bf16[16,128,128]{2,1,0:T(8,128)(2,1)} %get-tuple-element.7) | copy-start | bytes 1572868
  51.4 0.8 %copy-start.1 = (f32[1,2]{1,0:T(1,128)S(1)}, f32[1,2]{1,0:T(1,128)}, u32[]{:S(2)}) copy-start(f32[1,2]{1,0:T(1,128)} %get-tuple-element.8) | copy-start | bytes 28

commit v2 on v1

--- a/solution.py
+++ b/solution.py
@@ -70,16 +70,17 @@
 
 def kernel(
     sizes,
+    owner_hbm,
+    pool_hbm,
+    g_hbm,
+    m_hbm,
+    nm_ref,
+    out_ref,
+    slot_ref,
     owner_ref,
     pool_ref,
-    g_hbm,
-    m_hbm,
-    nm_hbm,
-    out_hbm,
-    slot_ref,
     gbuf,
     mbuf,
-    nmbuf,
     nes,
     yq,
     yr,
@@ -94,7 +95,6 @@
     sd,
     gram,
     qall,
-    outbuf,
     t0,
     t0r,
     t1,
@@ -102,8 +102,6 @@
     t2,
     t2r,
     in_sem,
-    nm_sem,
-    out_sem,
     z_send,
     z_recv,
     c_send,
@@ -130,6 +128,7 @@
     y = lax.div(f, NK)
     x = lax.div(k, 2)
     c = lax.rem(k, 2)
+    plane = lax.rem(k + NZ - z, NZ)
 
     def dev(yy, xx, cc, zz):
         return ((yy * NX + xx) * 2 + cc, zz)
@@ -146,13 +145,17 @@
         return dev(y, x, c, lax.rem(z + d, NZ))
 
     def wdev(d):
-        return (lax.rem(y + d, NY) * NK + z, k)
+        return (lax.rem(y + d, NY) * NK + k, plane)
 
     def remote(src, dst, send, recv, device):
         return pltpu.make_async_remote_copy(
             src_ref=src, dst_ref=dst, send_sem=send, recv_sem=recv, device_id=device, device_id_type=MESH
         )
 
+    own_copy = pltpu.make_async_copy(owner_hbm, owner_ref, in_sem.at[8])
+    pool_copy = pltpu.make_async_copy(pool_hbm, pool_ref, in_sem.at[9])
+    own_copy.start()
+    pool_copy.start()
     CHUNKS = 4
     per = NB // CHUNKS
     loads = []
@@ -177,11 +180,8 @@
         greet(xdev(d))
     greet(partner)
 
-    @pl.when(k != z)
-    def _():
-        for d in range(NY):
-            greet(wdev(d))
-
+    own_copy.wait()
+    pool_copy.wait()
     codes = [pool_ref[0, j] for j in range(NB)]
     source = []
     for q in range(NB):
@@ -190,19 +190,14 @@
             at = jnp.where(codes[j] == q, j, at)
         source.append(at)
 
-    stores = []
     for i in range(CHUNKS):
         for cp in loads[i]:
             cp.wait()
         for j in range(i * per, (i + 1) * per):
             grad = gbuf[j].astype(jnp.float32)
             velocity = momentum_rate * mbuf[j].astype(jnp.float32) + grad
-            nmbuf[j] = velocity.astype(jnp.bfloat16)
+            nm_ref[j] = velocity.astype(jnp.bfloat16)
             nes[j] = (grad + momentum_rate * velocity).astype(jnp.bfloat16)
-        part = pl.ds(i * per, per)
-        st = pltpu.make_async_copy(nmbuf.at[part], nm_hbm.at[part], nm_sem.at[i])
-        st.start()
-        stores.append(st)
 
     for p in range(NZ):
         grams = []
@@ -215,9 +210,10 @@
             grams.append(
                 lax.dot_general(value, value, (((1,), (1,)), ((), ())), preferred_element_type=jnp.float32)
             )
-        put_packed(pk.at[p % 2, p // 2], *grams)
-
-    pl.semaphore_wait(barrier, (NZ - 1) + (NY - 1) + (NX - 1) + 1 + jnp.where(k != z, NY, 0))
+        place = lax.rem(p + z, NK)
+        put_packed(pk.at[lax.rem(place, 2), lax.div(place, 2)], *grams)
+
+    pl.semaphore_wait(barrier, (NZ - 1) + (NY - 1) + (NX - 1) + 1 )
 
     sent = []
 
@@ -288,12 +284,12 @@
     l0 = pltpu.make_async_copy(s3, gram.at[own_rows], w_recv.at[0])
     l1 = pltpu.make_async_copy(sd, gram.at[pl.ds(H, 8)], w_recv.at[NY])
 
-    @pl.when(k != z)
+    @pl.when(plane != z)
     def _():
         w0.start()
         w1.start()
 
-    @pl.when(k == z)
+    @pl.when(plane == z)
     def _():
         l0.start()
         l1.start()
@@ -334,10 +330,10 @@
     for cp in zc:
         cp.wait_recv()
     factor = step_size * 0.2 * math.sqrt(H * NK * NY)
-    outs = []
-
-    def apply(slot, i):
-        for e, q in enumerate(get_packed(qall.at[slot])):
+
+    def apply(at):
+        slot = lax.rem(at + NZ - z, NZ)
+        for e, q in enumerate(get_packed(qall.at[at])):
             high = q.astype(jnp.bfloat16)
             rest = (q - high.astype(jnp.float32)).astype(jnp.bfloat16)
             value = yr[2 * slot + e]
@@ -346,31 +342,25 @@
                 jnp.concatenate([value, value], axis=0),
                 preferred_element_type=jnp.float32,
             ).astype(jnp.bfloat16)
-            outbuf[2 * slot + e] = (-factor * ortho.astype(jnp.float32)).astype(jnp.bfloat16)
-        part = pl.ds(2 * slot, 2)
-        st = pltpu.make_async_copy(outbuf.at[part], out_hbm.at[part], out_sem.at[i])
-        st.start()
-        outs.append(st)
-
-    apply(k, 0)
+            out_ref[2 * slot + e] = (-factor * ortho.astype(jnp.float32)).astype(jnp.bfloat16)
+
+    apply(k)
     b_own.wait_recv()
-    apply(2 * x + 1 - c, 1)
+    apply(2 * x + 1 - c)
     fwd = []
     for d in range(1, NX):
         xa[d - 1].wait_recv()
         slot = 2 * lax.rem(x + NX - d, NX) + c
         fwd.append(go(remote(qall.at[slot], qall.at[slot], b_send.at[d], b_recv.at[d], partner)))
-        apply(slot, 2 * d)
+        apply(slot)
     for d in range(1, NX):
         fwd[d - 1].wait_recv()
-        apply(2 * lax.rem(x + NX - d, NX) + 1 - c, 2 * d + 1)
-
-    for st in outs + stores:
-        st.wait()
+        apply(2 * lax.rem(x + NX - d, NX) + 1 - c)
+
     for cp in sent:
         cp.wait_send()
 
-    @pl.when(k != z)
+    @pl.when(plane != z)
     def _():
         w0.wait_send()
         w1.wait_send()
@@ -381,9 +371,10 @@
     NK = 2 * NX
     f32, bf16 = jnp.float32, jnp.bfloat16
     dma = pltpu.SemaphoreType.DMA
-    hbm = pl.BlockSpec(memory_space=pl.ANY)
+    hbm = pl.BlockSpec(memory_space=pltpu.HBM)
     scratch = [
-        pltpu.VMEM((NB, H, H), bf16),
+        pltpu.SMEM((1, NB), jnp.int32),
+        pltpu.SMEM((1, NB), jnp.int32),
         pltpu.VMEM((NB, H, H), bf16),
         pltpu.VMEM((NB, H, H), bf16),
         pltpu.VMEM((NB, H, H), bf16),
@@ -400,16 +391,13 @@
         pltpu.VMEM((8, H), f32),
         pltpu.VMEM((PACKED, H), f32),
         pltpu.VMEM((NK, PACKED, H), f32),
-        pltpu.VMEM((NB, H, H), bf16),
         pltpu.VMEM((NB, H), f32),
         pltpu.VMEM((NB, H), f32),
         pltpu.VMEM((NB, H), f32),
         pltpu.VMEM((NX - 1, NB, H), f32),
         pltpu.VMEM((NB, H), f32),
         pltpu.VMEM((NY, NB, H), f32),
-        dma((8,)),
-        dma((4,)),
-        dma((NK,)),
+        dma((10,)),
         dma((NZ,)),
         dma((NZ,)),
         dma((2,)),
@@ -427,7 +415,6 @@
         dma((NX,)),
         dma((NX,)),
     ]
-    smem = pl.BlockSpec(memory_space=pltpu.SMEM)
     return pl.pallas_call(
         functools.partial(kernel, sizes),
         out_shape=(
@@ -435,13 +422,18 @@
             jax.ShapeDtypeStruct(grads.shape, bf16),
             jax.ShapeDtypeStruct((1, 2), f32),
         ),
-        in_specs=[smem, smem, hbm, hbm],
-        out_specs=(hbm, hbm, pl.BlockSpec(memory_space=pltpu.VMEM)),
+        in_specs=[hbm] * 4,
+        out_specs=(pl.BlockSpec(memory_space=pltpu.VMEM),) * 3,
         scratch_shapes=scratch,
         compiler_params=pltpu.CompilerParams(
-            collective_id=0, has_side_effects=True
+            collective_id=0, has_side_effects=True, vmem_limit_bytes=24 * 1024 * 1024
         ),
-    )(owner_table.reshape(1, NB), pool_map, grads, momentum)
+    )(
+        *(
+            pltpu.with_memory_space_constraint(v, pltpu.HBM)
+            for v in (owner_table.reshape(1, NB), pool_map, grads, momentum)
+        )
+    )
 
 
 def solution(mesh, sizes=(4, 8, 8, 16)):

time: 52.8 us -> 46.6 us (0.88)
  Pallas kernels: 48.8 us -> 43.7 us
  local copies, waits for them, and re-layouts: 3.25 us -> 2.1 us
    pallas_call x1, Pallas kernels: 48.8 us -> 43.7 us  [local(): pl.pallas_call(functools.partial(kernel, sizes), out_shape=(jax.ShapeDtyp...]
    unnamed x7 -> x3, local copies, waits for them, and re-layouts: 3.25 us -> 2.1 us
where the time goes in v2:
time: 46.6 us; the launch traced here: 46.4 us
  Pallas kernels  43.7 us (94%)
  local copies, waits for them, and re-layouts  2.1 us (5%)
  between operations  0.64 us (1%)
    pallas_call x1, Pallas kernels, local(): pl.pallas_call(functools.partial(kernel, sizes), out_shape=(jax.ShapeDtyp...  43.7 us
    unnamed x3, local copies, waits for them, and re-layouts  2.1 us

profile of v2, /device:TPU:1, one launch (start us, length us, event | category | flops | bytes accessed | tf_op | source)
XLA Modules:
  0.0 46.4 jit_solution(10343137512603360517)
XLA Ops:
  0.6 43.7 %shard_map.67 = (bf16[16,128,128]{2,1,0:T(8,128)(2,1)S(1)}, bf16[16,128,128]{2,1,0:T(8,128)(2,1)S(1)}, f32[1,2]{1,0:T(1,128)S(1)}) custom-call(s32[1,16]{1,0:T(1,128)} %bitcast.1, s32[1,16]{1,0:T(1,128)} %pool_hbm.1, bf16[16,128,128]{2,1,0:T(8,128)(2,1)} %g_hbm.1, bf16[16,128,128]{2,1,0:T(8,128)(2,1)} %m_hbm.1), custom_call_target="tpu_custom_call" | custom-call | tf_op jit(solution)/shard_map/pallas_call | solution.py:418
  44.3 0.8 %copy.10 = bf16[16,128,128]{2,1,0:T(8,128)(2,1)} copy(bf16[16,128,128]{2,1,0:T(8,128)(2,1)S(1)} %get-tuple-element.6) | data formatting | bytes 1048576
  45.1 0.8 %copy.11 = bf16[16,128,128]{2,1,0:T(8,128)(2,1)} copy(bf16[16,128,128]{2,1,0:T(8,128)(2,1)S(1)} %get-tuple-element.7) | data formatting | bytes 1048576
  45.9 0.5 %copy.12 = f32[1,2]{1,0:T(1,128)} copy(f32[1,2]{1,0:T(1,128)S(1)} %get-tuple-element.8) | data formatting | bytes 16

commit v3 on v2

--- a/solution.py
+++ b/solution.py
@@ -81,7 +81,6 @@
     pool_ref,
     gbuf,
     mbuf,
-    nes,
     yq,
     yr,
     pk,
@@ -183,37 +182,35 @@
     own_copy.wait()
     pool_copy.wait()
     codes = [pool_ref[0, j] for j in range(NB)]
-    source = []
-    for q in range(NB):
+
+    def source(q):
         at = jnp.int32(0)
         for j in range(1, NB):
             at = jnp.where(codes[j] == q, j, at)
-        source.append(at)
-
-    for i in range(CHUNKS):
-        for cp in loads[i]:
+        return at
+
+    for pair in loads:
+        for cp in pair:
             cp.wait()
-        for j in range(i * per, (i + 1) * per):
-            grad = gbuf[j].astype(jnp.float32)
-            velocity = momentum_rate * mbuf[j].astype(jnp.float32) + grad
-            nm_ref[j] = velocity.astype(jnp.bfloat16)
-            nes[j] = (grad + momentum_rate * velocity).astype(jnp.bfloat16)
-
-    for p in range(NZ):
+
+    def nesterov(j):
+        grad = gbuf[j].astype(jnp.float32)
+        velocity = momentum_rate * mbuf[j].astype(jnp.float32) + grad
+        return velocity, (grad + momentum_rate * velocity).astype(jnp.bfloat16)
+
+    def make_pair(core, at):
+        p = lax.rem(2 * at + core + NZ - z, NZ)
         grams = []
         for e in range(2):
             q = 2 * p + e
-            value = nes[source[q]]
+            _, value = nesterov(source(q))
             yq[q] = value
             wide = value.astype(jnp.float32)
-            t0[q : q + 1, :] = jnp.sum(wide * wide, axis=0, keepdims=True)
+            t0[pl.ds(q, 1), :] = jnp.sum(wide * wide, axis=0, keepdims=True)
             grams.append(
                 lax.dot_general(value, value, (((1,), (1,)), ((), ())), preferred_element_type=jnp.float32)
             )
-        place = lax.rem(p + z, NK)
-        put_packed(pk.at[lax.rem(place, 2), lax.div(place, 2)], *grams)
-
-    pl.semaphore_wait(barrier, (NZ - 1) + (NY - 1) + (NX - 1) + 1 )
+        put_packed(pk.at[core, at], *grams)
 
     sent = []
 
@@ -222,8 +219,43 @@
         sent.append(copy)
         return copy
 
-    cc = go(remote(pk.at[1 - c], r0, c_send.at[0], c_recv.at[0], partner))
-    ct = go(remote(t0, t0r, c_send.at[1], c_recv.at[1], partner))
+    left, right, far = lax.rem(x + NX - 1, NX), lax.rem(x + 1, NX), lax.rem(x + 2, NX)
+    order = [far, left, right, x]
+    cc = []
+    for i, at in enumerate(order):
+        make_pair(1 - c, at)
+        if i == 0:
+            pl.semaphore_wait(barrier, (NZ - 1) + (NY - 1) + (NX - 1) + 1)
+        cc.append(go(remote(pk.at[1 - c, at], r0.at[at], c_send.at[i], c_recv.at[i], partner)))
+    for at in order:
+        make_pair(c, at)
+    ct = go(remote(t0, t0r, c_send.at[NX], c_recv.at[NX], partner))
+
+    upper, lower = pl.ds(0, H // 2), pl.ds(H // 2, PACKED - H // 2)
+    to_right = {"device": dev(y, right, c, z)}
+    to_left = {"device": dev(y, left, c, z)}
+    cc[0].wait_recv()
+    s1[far] = pk[c, far] + r0[far]
+    f_up = go(remote(s1.at[far, upper], r1.at[0, upper], x_send.at[0], x_recv.at[0], **to_right))
+    f_low = go(remote(s1.at[far, lower], r1.at[0, lower], x_send.at[1], x_recv.at[1], **to_left))
+    cc[1].wait_recv()
+    s1[left] = pk[c, left] + r0[left]
+    d_up = go(remote(s1.at[left, upper], r1.at[1, upper], x_send.at[2], x_recv.at[2], **to_left))
+    cc[2].wait_recv()
+    s1[right] = pk[c, right] + r0[right]
+    d_low = go(remote(s1.at[right, lower], r1.at[1, lower], x_send.at[3], x_recv.at[3], **to_right))
+    ct.wait_recv()
+    t1[...] = t0[...] + t0r[...]
+    tx = [go(remote(t1, t1r.at[d - 1], t_send.at[d], t_recv.at[d], xdev(d))) for d in range(1, NX)]
+    cc[3].wait_recv()
+    s1[x] = pk[c, x] + r0[x]
+    f_up.wait_recv()
+    r0[0, upper, :] = s1[right, upper, :] + r1[0, upper, :]
+    g_up = go(remote(r0.at[0, upper], r1.at[2, upper], x_send.at[4], x_recv.at[4], **to_right))
+    f_low.wait_recv()
+    r0[0, lower, :] = s1[left, lower, :] + r1[0, lower, :]
+    g_low = go(remote(r0.at[0, lower], r1.at[2, lower], x_send.at[5], x_recv.at[5], **to_left))
+
     zc = []
     for d in sorted(range(1, NZ), key=lambda d: -min(d, NZ - d)):
         to = lax.rem(z + d, NZ)
@@ -231,23 +263,12 @@
     mine = pltpu.make_async_copy(yq.at[pl.ds(2 * z, 2)], yr.at[pl.ds(2 * z, 2)], z_recv.at[0])
     mine.start()
 
-    cc.wait_recv()
-    for i in range(NX):
-        s1[i] = pk[c, i] + r0[i]
-    xc = []
-    for d in range(1, NX):
-        to = lax.rem(x + d, NX)
-        xc.append(go(remote(s1.at[to], r1.at[d - 1], x_send.at[d], x_recv.at[d], xdev(d))))
-    ct.wait_recv()
-    t1[...] = t0[...] + t0r[...]
-    tx = [go(remote(t1, t1r.at[d - 1], t_send.at[d], t_recv.at[d], xdev(d))) for d in range(1, NX)]
-
-    for cp in xc:
-        cp.wait_recv()
-    total = s1[x]
-    for d in range(1, NX):
-        total = total + r1[d - 1]
-    s2[...] = total
+    for j in range(NB):
+        nm_ref[j] = nesterov(j)[0].astype(jnp.bfloat16)
+
+    for cp in (d_up, d_low, g_up, g_low):
+        cp.wait_recv()
+    s2[...] = s1[x] + r1[1] + r1[2]
     yc, yd = [], []
     for d in sorted(range(1, NY), key=lambda d: -min(d, NY - d)):
         to = lax.rem(y + d, NY)
@@ -321,10 +342,16 @@
     a, b = newton_schulz(list(get_packed(gram)))
     put_packed(qall.at[k], a, b)
 
-    xa = []
     b_own = go(remote(qall.at[k], qall.at[k], b_send.at[0], b_recv.at[0], partner))
-    for d in range(1, NX):
-        xa.append(go(remote(qall.at[k], qall.at[k], a_send.at[d], a_recv.at[d], xdev(d))))
+
+    def pass_on(at, rows, i, device):
+        return go(remote(qall.at[at, rows], qall.at[at, rows], a_send.at[i], a_recv.at[i], device))
+
+    k_left, k_right, k_far = 2 * left + c, 2 * right + c, 2 * far + c
+    up_right = pass_on(k, upper, 0, to_right["device"])
+    low_left = pass_on(k, lower, 1, to_left["device"])
+    low_right = pass_on(k, lower, 2, to_right["device"])
+    up_left = pass_on(k, upper, 3, to_left["device"])
 
     mine.wait()
     for cp in zc:
@@ -344,18 +371,32 @@
             ).astype(jnp.bfloat16)
             out_ref[2 * slot + e] = (-factor * ortho.astype(jnp.float32)).astype(jnp.bfloat16)
 
+    def across(at, i):
+        return go(remote(qall.at[at], qall.at[at], b_send.at[i], b_recv.at[i], partner))
+
     apply(k)
+    up_right.wait_recv()
+    far_up = pass_on(k_left, upper, 4, to_right["device"])
+    low_left.wait_recv()
+    far_low = pass_on(k_right, lower, 5, to_left["device"])
     b_own.wait_recv()
     apply(2 * x + 1 - c)
-    fwd = []
-    for d in range(1, NX):
-        xa[d - 1].wait_recv()
-        slot = 2 * lax.rem(x + NX - d, NX) + c
-        fwd.append(go(remote(qall.at[slot], qall.at[slot], b_send.at[d], b_recv.at[d], partner)))
-        apply(slot)
-    for d in range(1, NX):
-        fwd[d - 1].wait_recv()
-        apply(2 * lax.rem(x + NX - d, NX) + 1 - c)
+    low_right.wait_recv()
+    b_left = across(k_left, 1)
+    up_left.wait_recv()
+    b_right = across(k_right, 2)
+    apply(k_left)
+    apply(k_right)
+    far_up.wait_recv()
+    far_low.wait_recv()
+    b_far = across(k_far, 3)
+    b_left.wait_recv()
+    apply(2 * left + 1 - c)
+    b_right.wait_recv()
+    apply(2 * right + 1 - c)
+    apply(k_far)
+    b_far.wait_recv()
+    apply(2 * far + 1 - c)
 
     for cp in sent:
         cp.wait_send()
@@ -364,6 +405,26 @@
     def _():
         w0.wait_send()
         w1.wait_send()
+
+
+def writer(*refs):
+    copies = [pltpu.make_async_copy(refs[i], refs[3 + i], refs[6].at[i]) for i in range(3)]
+    for cp in copies:
+        cp.start()
+    for cp in copies:
+        cp.wait()
+
+
+def written(results):
+    vmem = pl.BlockSpec(memory_space=pltpu.VMEM)
+    return pl.pallas_call(
+        writer,
+        out_shape=tuple(jax.ShapeDtypeStruct(v.shape, v.dtype) for v in results),
+        in_specs=[vmem] * 3,
+        out_specs=(pl.BlockSpec(memory_space=pltpu.HBM),) * 3,
+        scratch_shapes=[pltpu.SemaphoreType.DMA((3,))],
+        compiler_params=pltpu.CompilerParams(vmem_limit_bytes=8 * 1024 * 1024),
+    )(*results)
 
 
 def local(sizes, grads, momentum, owner_table, pool_map):
@@ -375,7 +436,6 @@
     scratch = [
         pltpu.SMEM((1, NB), jnp.int32),
         pltpu.SMEM((1, NB), jnp.int32),
-        pltpu.VMEM((NB, H, H), bf16),
         pltpu.VMEM((NB, H, H), bf16),
         pltpu.VMEM((NB, H, H), bf16),
         pltpu.VMEM((NB, H, H), bf16),
@@ -400,22 +460,22 @@
         dma((10,)),
         dma((NZ,)),
         dma((NZ,)),
-        dma((2,)),
-        dma((2,)),
-        dma((NX,)),
-        dma((NX,)),
+        dma((NX + 1,)),
+        dma((NX + 1,)),
+        dma((6,)),
+        dma((6,)),
         dma((2 * NY,)),
         dma((2 * NY,)),
         dma((NX + NY,)),
         dma((NX + NY,)),
         dma((NY + 1,)),
         dma((NY + 1,)),
-        dma((NX,)),
-        dma((NX,)),
+        dma((6,)),
+        dma((6,)),
         dma((NX,)),
         dma((NX,)),
     ]
-    return pl.pallas_call(
+    results = pl.pallas_call(
         functools.partial(kernel, sizes),
         out_shape=(
             jax.ShapeDtypeStruct(grads.shape, bf16),
@@ -434,6 +494,7 @@
             for v in (owner_table.reshape(1, NB), pool_map, grads, momentum)
         )
     )
+    return written(results)
 
 
 def solution(mesh, sizes=(4, 8, 8, 16)):

time: 46.6 us -> 47.9 us (1.028)
  Pallas kernels: 43.7 us -> 47.1 us
  local copies, waits for them, and re-layouts: 2.1 us -> 0 us
    pallas_call x1, Pallas kernels: 43.7 us -> 46.1 us  [local(): pl.pallas_call(functools.partial(kernel, sizes), out_shape=(jax.ShapeDtyp...]
    unnamed x3 -> x0, local copies, waits for them, and re-layouts: 2.1 us -> none
    pallas_call x0 -> x1, Pallas kernels: none -> 1 us  [written(): pl.pallas_call(writer, out_shape=tuple((jax.ShapeDtypeStruct(v.shape, v.d...]
where the time goes in v3:
time: 47.9 us; the launch traced here: 47.7 us
  Pallas kernels  47.1 us (98%)
  between operations  0.64 us (1%)
    pallas_call x1, Pallas kernels, local(): pl.pallas_call(functools.partial(kernel, sizes), out_shape=(jax.ShapeDtyp...  46.1 us
    pallas_call x1, Pallas kernels, written(): pl.pallas_call(writer, out_shape=tuple((jax.ShapeDtypeStruct(v.shape, v.d...  1 us

profile of v3, /device:TPU:1, one launch (start us, length us, event | category | flops | bytes accessed | tf_op | source)
XLA Modules:
  0.0 47.7 jit_solution(16152159309772516333)
XLA Ops:
  0.6 46.1 %shard_map.67 = (bf16[16,128,128]{2,1,0:T(8,128)(2,1)S(1)}, bf16[16,128,128]{2,1,0:T(8,128)(2,1)S(1)}, f32[1,2]{1,0:T(1,128)S(1)}) custom-call(s32[1,16]{1,0:T(1,128)} %bitcast.1, s32[1,16]{1,0:T(1,128)} %pool_hbm.1, bf16[16,128,128]{2,1,0:T(8,128)(2,1)} %g_hbm.1, bf16[16,128,128]{2,1,0:T(8,128)(2,1)} %m_hbm.1), custom_call_target="tpu_custom_call" | custom-call | tf_op jit(solution)/shard_map/pallas_call | solution.py:478
  46.8 1.0 %shard_map.68 = (bf16[16,128,128]{2,1,0:T(8,128)(2,1)}, bf16[16,128,128]{2,1,0:T(8,128)(2,1)}, f32[1,2]{1,0:T(1,128)}) custom-call(bf16[16,128,128]{2,1,0:T(8,128)(2,1)S(1)} %get-tuple-element.6.refs_0_, bf16[16,128,128]{2,1,0:T(8,128)(2,1)S(1)} %get-tuple-element.7.refs_1_, f32[1,2]{1,0:T(1,128)S(1)} %get-tuple-element.8.refs_2_), custom_call_target="tpu_custom_call" | custom-call | tf_op jit(solution)/shard_map/pallas_call | solution.py:420

commit v4 on v3

--- a/solution.py
+++ b/solution.py
@@ -128,6 +128,7 @@
     x = lax.div(k, 2)
     c = lax.rem(k, 2)
     plane = lax.rem(k + NZ - z, NZ)
+    k_far = lax.rem(k + NX, NK)
 
     def dev(yy, xx, cc, zz):
         return ((yy * NX + xx) * 2 + cc, zz)
@@ -143,8 +144,8 @@
     def zdev(d):
         return dev(y, x, c, lax.rem(z + d, NZ))
 
-    def wdev(d):
-        return (lax.rem(y + d, NY) * NK + k, plane)
+    def wdev(d, across_x):
+        return (lax.rem(y + d, NY) * NK + (k_far if across_x else k), plane)
 
     def remote(src, dst, send, recv, device):
         return pltpu.make_async_remote_copy(
@@ -230,6 +231,13 @@
     for at in order:
         make_pair(c, at)
     ct = go(remote(t0, t0r, c_send.at[NX], c_recv.at[NX], partner))
+
+    zc = []
+    for d in sorted(range(1, NZ), key=lambda d: -min(d, NZ - d)):
+        to = lax.rem(z + d, NZ)
+        zc.append(go(remote(yq.at[pl.ds(2 * to, 2)], yr.at[pl.ds(2 * z, 2)], z_send.at[d], z_recv.at[d], zdev(d))))
+    mine = pltpu.make_async_copy(yq.at[pl.ds(2 * z, 2)], yr.at[pl.ds(2 * z, 2)], z_recv.at[0])
+    mine.start()
 
     upper, lower = pl.ds(0, H // 2), pl.ds(H // 2, PACKED - H // 2)
     to_right = {"device": dev(y, right, c, z)}
@@ -256,13 +264,6 @@
     r0[0, lower, :] = s1[left, lower, :] + r1[0, lower, :]
     g_low = go(remote(r0.at[0, lower], r1.at[2, lower], x_send.at[5], x_recv.at[5], **to_left))
 
-    zc = []
-    for d in sorted(range(1, NZ), key=lambda d: -min(d, NZ - d)):
-        to = lax.rem(z + d, NZ)
-        zc.append(go(remote(yq.at[pl.ds(2 * to, 2)], yr.at[pl.ds(2 * z, 2)], z_send.at[d], z_recv.at[d], zdev(d))))
-    mine = pltpu.make_async_copy(yq.at[pl.ds(2 * z, 2)], yr.at[pl.ds(2 * z, 2)], z_recv.at[0])
-    mine.start()
-
     for j in range(NB):
         nm_ref[j] = nesterov(j)[0].astype(jnp.bfloat16)
 
@@ -293,17 +294,23 @@
     own_rows = pl.ds(pl.multiple_of(y * CH, CH), CH)
     wc = []
     for d in sorted(range(1, NY), key=lambda d: -min(d, NY - d)):
-        wc.append(go(remote(s3, gram.at[own_rows], w_send.at[d], w_recv.at[d], wdev(d))))
+        for i in (1, 0):
+            wc.append(
+                go(remote(s3, gram.at[i, own_rows], w_send.at[i, d], w_recv.at[i, d], wdev(d, i)))
+            )
+    wc.append(go(remote(s3, gram.at[1, own_rows], w_send.at[1, 0], w_recv.at[1, 0], wdev(0, 1))))
     for cp in yd:
         cp.wait_recv()
     total = s2[pl.ds(H, 8), :]
     for d in range(1, NY):
         total = total + rd[d - 1]
     sd[...] = total
-    w0 = remote(s3, gram.at[own_rows], w_send.at[0], w_recv.at[0], wdev(0))
-    w1 = remote(sd, gram.at[pl.ds(H, 8)], w_send.at[NY], w_recv.at[NY], wdev(0))
-    l0 = pltpu.make_async_copy(s3, gram.at[own_rows], w_recv.at[0])
-    l1 = pltpu.make_async_copy(sd, gram.at[pl.ds(H, 8)], w_recv.at[NY])
+    last = pl.ds(H, 8)
+    wc.append(go(remote(sd, gram.at[1, last], w_send.at[1, NY], w_recv.at[1, NY], wdev(0, 1))))
+    w0 = remote(s3, gram.at[0, own_rows], w_send.at[0, 0], w_recv.at[0, 0], wdev(0, 0))
+    w1 = remote(sd, gram.at[0, last], w_send.at[0, NY], w_recv.at[0, NY], wdev(0, 0))
+    l0 = pltpu.make_async_copy(s3, gram.at[0, own_rows], w_recv.at[0, 0])
+    l1 = pltpu.make_async_copy(sd, gram.at[0, last], w_recv.at[0, NY])
 
     @pl.when(plane != z)
     def _():
@@ -339,19 +346,18 @@
         cp.wait_recv()
     l0.wait()
     l1.wait()
-    a, b = newton_schulz(list(get_packed(gram)))
-    put_packed(qall.at[k], a, b)
-
-    b_own = go(remote(qall.at[k], qall.at[k], b_send.at[0], b_recv.at[0], partner))
-
-    def pass_on(at, rows, i, device):
-        return go(remote(qall.at[at, rows], qall.at[at, rows], a_send.at[i], a_recv.at[i], device))
-
-    k_left, k_right, k_far = 2 * left + c, 2 * right + c, 2 * far + c
-    up_right = pass_on(k, upper, 0, to_right["device"])
-    low_left = pass_on(k, lower, 1, to_left["device"])
-    low_right = pass_on(k, lower, 2, to_right["device"])
-    up_left = pass_on(k, upper, 3, to_left["device"])
+    qs = newton_schulz([*get_packed(gram.at[0]), *get_packed(gram.at[1])])
+    put_packed(qall.at[k], qs[0], qs[1])
+
+    def across(at, i):
+        return go(remote(qall.at[at], qall.at[at], b_send.at[i], b_recv.at[i], partner))
+
+    k_left, k_right = 2 * left + c, 2 * right + c
+    from_left = go(remote(qall.at[k], qall.at[k], a_send.at[0], a_recv.at[0], to_right["device"]))
+    from_right = go(remote(qall.at[k], qall.at[k], a_send.at[1], a_recv.at[1], to_left["device"]))
+    b_own = across(k, 0)
+    put_packed(qall.at[k_far], qs[2], qs[3])
+    b_far = across(k_far, 1)
 
     mine.wait()
     for cp in zc:
@@ -371,32 +377,22 @@
             ).astype(jnp.bfloat16)
             out_ref[2 * slot + e] = (-factor * ortho.astype(jnp.float32)).astype(jnp.bfloat16)
 
-    def across(at, i):
-        return go(remote(qall.at[at], qall.at[at], b_send.at[i], b_recv.at[i], partner))
-
     apply(k)
-    up_right.wait_recv()
-    far_up = pass_on(k_left, upper, 4, to_right["device"])
-    low_left.wait_recv()
-    far_low = pass_on(k_right, lower, 5, to_left["device"])
+    apply(k_far)
     b_own.wait_recv()
     apply(2 * x + 1 - c)
-    low_right.wait_recv()
-    b_left = across(k_left, 1)
-    up_left.wait_recv()
-    b_right = across(k_right, 2)
+    b_far.wait_recv()
+    apply(2 * far + 1 - c)
+    from_left.wait_recv()
+    b_left = across(k_left, 2)
+    from_right.wait_recv()
+    b_right = across(k_right, 3)
     apply(k_left)
     apply(k_right)
-    far_up.wait_recv()
-    far_low.wait_recv()
-    b_far = across(k_far, 3)
     b_left.wait_recv()
     apply(2 * left + 1 - c)
     b_right.wait_recv()
     apply(2 * right + 1 - c)
-    apply(k_far)
-    b_far.wait_recv()
-    apply(2 * far + 1 - c)
 
     for cp in sent:
         cp.wait_send()
@@ -449,7 +445,7 @@
         pltpu.VMEM((NY - 1, 8, H), f32),
         pltpu.VMEM((H // NY, H), f32),
         pltpu.VMEM((8, H), f32),
-        pltpu.VMEM((PACKED, H), f32),
+        pltpu.VMEM((2, PACKED, H), f32),
         pltpu.VMEM((NK, PACKED, H), f32),
         pltpu.VMEM((NB, H), f32),
         pltpu.VMEM((NB, H), f32),
@@ -468,10 +464,10 @@
         dma((2 * NY,)),
         dma((NX + NY,)),
         dma((NX + NY,)),
-        dma((NY + 1,)),
-        dma((NY + 1,)),
-        dma((6,)),
-        dma((6,)),
+        dma((2, NY + 1)),
+        dma((2, NY + 1)),
+        dma((2,)),
+        dma((2,)),
         dma((NX,)),
         dma((NX,)),
     ]

time: 47.9 us -> 47.6 us (level)
  no operation moved by 1% of the time
where the time goes in v4:
time: 47.6 us; the launch traced here: 47.4 us
  Pallas kernels  46.8 us (98%)
  between operations  0.64 us (1%)
    pallas_call x1, Pallas kernels, local(): pl.pallas_call(functools.partial(kernel, sizes), out_shape=(jax.ShapeDtyp...  45.8 us
    pallas_call x1, Pallas kernels, written(): pl.pallas_call(writer, out_shape=tuple((jax.ShapeDtypeStruct(v.shape, v.d...  1 us

profile of v4, /device:TPU:1, one launch (start us, length us, event | category | flops | bytes accessed | tf_op | source)
XLA Modules:
  0.0 47.4 jit_solution(6542370198007535678)
XLA Ops:
  0.6 45.8 %shard_map.67 = (bf16[16,128,128]{2,1,0:T(8,128)(2,1)S(1)}, bf16[16,128,128]{2,1,0:T(8,128)(2,1)S(1)}, f32[1,2]{1,0:T(1,128)S(1)}) custom-call(s32[1,16]{1,0:T(1,128)} %bitcast.1, s32[1,16]{1,0:T(1,128)} %pool_hbm.1, bf16[16,128,128]{2,1,0:T(8,128)(2,1)} %g_hbm.1, bf16[16,128,128]{2,1,0:T(8,128)(2,1)} %m_hbm.1), custom_call_target="tpu_custom_call" | custom-call | tf_op jit(solution)/shard_map/pallas_call | solution.py:474
  46.4 1.0 %shard_map.68 = (bf16[16,128,128]{2,1,0:T(8,128)(2,1)}, bf16[16,128,128]{2,1,0:T(8,128)(2,1)}, f32[1,2]{1,0:T(1,128)}) custom-call(bf16[16,128,128]{2,1,0:T(8,128)(2,1)S(1)} %get-tuple-element.6.refs_0_, bf16[16,128,128]{2,1,0:T(8,128)(2,1)S(1)} %get-tuple-element.7.refs_1_, f32[1,2]{1,0:T(1,128)S(1)} %get-tuple-element.8.refs_2_), custom_call_target="tpu_custom_call" | custom-call | tf_op jit(solution)/shard_map/pallas_call | solution.py:416

commit v5 on v3

--- a/solution.py
+++ b/solution.py
@@ -44,8 +44,18 @@
     return a, b
 
 
+def halves(v):
+    high = v.astype(jnp.bfloat16)
+    return high, (v - high.astype(jnp.float32)).astype(jnp.bfloat16)
+
+
 def dot32(a, b):
-    return jnp.dot(a, b, precision=lax.Precision.HIGHEST, preferred_element_type=jnp.float32)
+    (ah, al), (bh, bl) = halves(a), halves(b)
+    return jnp.dot(
+        jnp.concatenate([ah, al, ah], axis=1),
+        jnp.concatenate([bh, bh, bl], axis=0),
+        preferred_element_type=jnp.float32,
+    )
 
 
 def newton_schulz(grams):
@@ -231,31 +241,6 @@
         make_pair(c, at)
     ct = go(remote(t0, t0r, c_send.at[NX], c_recv.at[NX], partner))
 
-    upper, lower = pl.ds(0, H // 2), pl.ds(H // 2, PACKED - H // 2)
-    to_right = {"device": dev(y, right, c, z)}
-    to_left = {"device": dev(y, left, c, z)}
-    cc[0].wait_recv()
-    s1[far] = pk[c, far] + r0[far]
-    f_up = go(remote(s1.at[far, upper], r1.at[0, upper], x_send.at[0], x_recv.at[0], **to_right))
-    f_low = go(remote(s1.at[far, lower], r1.at[0, lower], x_send.at[1], x_recv.at[1], **to_left))
-    cc[1].wait_recv()
-    s1[left] = pk[c, left] + r0[left]
-    d_up = go(remote(s1.at[left, upper], r1.at[1, upper], x_send.at[2], x_recv.at[2], **to_left))
-    cc[2].wait_recv()
-    s1[right] = pk[c, right] + r0[right]
-    d_low = go(remote(s1.at[right, lower], r1.at[1, lower], x_send.at[3], x_recv.at[3], **to_right))
-    ct.wait_recv()
-    t1[...] = t0[...] + t0r[...]
-    tx = [go(remote(t1, t1r.at[d - 1], t_send.at[d], t_recv.at[d], xdev(d))) for d in range(1, NX)]
-    cc[3].wait_recv()
-    s1[x] = pk[c, x] + r0[x]
-    f_up.wait_recv()
-    r0[0, upper, :] = s1[right, upper, :] + r1[0, upper, :]
-    g_up = go(remote(r0.at[0, upper], r1.at[2, upper], x_send.at[4], x_recv.at[4], **to_right))
-    f_low.wait_recv()
-    r0[0, lower, :] = s1[left, lower, :] + r1[0, lower, :]
-    g_low = go(remote(r0.at[0, lower], r1.at[2, lower], x_send.at[5], x_recv.at[5], **to_left))
-
     zc = []
     for d in sorted(range(1, NZ), key=lambda d: -min(d, NZ - d)):
         to = lax.rem(z + d, NZ)
@@ -263,12 +248,27 @@
     mine = pltpu.make_async_copy(yq.at[pl.ds(2 * z, 2)], yr.at[pl.ds(2 * z, 2)], z_recv.at[0])
     mine.start()
 
+    upper, lower = pl.ds(0, H // 2), pl.ds(H // 2, PACKED - H // 2)
+    to_right = {"device": dev(y, right, c, z)}
+    to_left = {"device": dev(y, left, c, z)}
+    xc = []
+    for i, d in enumerate((2, 3, 1)):
+        cc[i].wait_recv()
+        at = order[i]
+        s1[at] = pk[c, at] + r0[at]
+        xc.append(go(remote(s1.at[at], r1.at[d - 1], x_send.at[d], x_recv.at[d], xdev(d))))
+    ct.wait_recv()
+    t1[...] = t0[...] + t0r[...]
+    tx = [go(remote(t1, t1r.at[d - 1], t_send.at[d], t_recv.at[d], xdev(d))) for d in range(1, NX)]
+    cc[3].wait_recv()
+    s1[x] = pk[c, x] + r0[x]
+
     for j in range(NB):
         nm_ref[j] = nesterov(j)[0].astype(jnp.bfloat16)
 
-    for cp in (d_up, d_low, g_up, g_low):
-        cp.wait_recv()
-    s2[...] = s1[x] + r1[1] + r1[2]
+    for cp in xc:
+        cp.wait_recv()
+    s2[...] = s1[x] + r1[0] + r1[1] + r1[2]
     yc, yd = [], []
     for d in sorted(range(1, NY), key=lambda d: -min(d, NY - d)):
         to = lax.rem(y + d, NY)
@@ -343,15 +343,9 @@
     put_packed(qall.at[k], a, b)
 
     b_own = go(remote(qall.at[k], qall.at[k], b_send.at[0], b_recv.at[0], partner))
-
-    def pass_on(at, rows, i, device):
-        return go(remote(qall.at[at, rows], qall.at[at, rows], a_send.at[i], a_recv.at[i], device))
-
-    k_left, k_right, k_far = 2 * left + c, 2 * right + c, 2 * far + c
-    up_right = pass_on(k, upper, 0, to_right["device"])
-    low_left = pass_on(k, lower, 1, to_left["device"])
-    low_right = pass_on(k, lower, 2, to_right["device"])
-    up_left = pass_on(k, upper, 3, to_left["device"])
+    xa = {}
+    for d in (2, 1, 3):
+        xa[d] = go(remote(qall.at[k], qall.at[k], a_send.at[d], a_recv.at[d], xdev(d)))
 
     mine.wait()
     for cp in zc:
@@ -375,28 +369,17 @@
         return go(remote(qall.at[at], qall.at[at], b_send.at[i], b_recv.at[i], partner))
 
     apply(k)
-    up_right.wait_recv()
-    far_up = pass_on(k_left, upper, 4, to_right["device"])
-    low_left.wait_recv()
-    far_low = pass_on(k_right, lower, 5, to_left["device"])
     b_own.wait_recv()
     apply(2 * x + 1 - c)
-    low_right.wait_recv()
-    b_left = across(k_left, 1)
-    up_left.wait_recv()
-    b_right = across(k_right, 2)
-    apply(k_left)
-    apply(k_right)
-    far_up.wait_recv()
-    far_low.wait_recv()
-    b_far = across(k_far, 3)
-    b_left.wait_recv()
-    apply(2 * left + 1 - c)
-    b_right.wait_recv()
-    apply(2 * right + 1 - c)
-    apply(k_far)
-    b_far.wait_recv()
-    apply(2 * far + 1 - c)
+    fwd = {}
+    for d in (1, 3, 2):
+        xa[d].wait_recv()
+        at = 2 * lax.rem(x + NX - d, NX) + c
+        fwd[d] = go(remote(qall.at[at], qall.at[at], b_send.at[d], b_recv.at[d], partner))
+        apply(at)
+    for d in (1, 3, 2):
+        fwd[d].wait_recv()
+        apply(2 * lax.rem(x + NX - d, NX) + 1 - c)
 
     for cp in sent:
         cp.wait_send()

time: 47.9 us -> 44.4 us (0.927)
  Pallas kernels: 47.1 us -> 43.6 us
    pallas_call x1, Pallas kernels: 46.1 us -> 42.6 us  [local(): pl.pallas_call(functools.partial(kernel, sizes), out_shape=(jax.ShapeDtyp...]
where the time goes in v5:
time: 44.4 us; the launch traced here: 44.3 us
  Pallas kernels  43.6 us (98%)
  between operations  0.64 us (1%)
    pallas_call x1, Pallas kernels, local(): pl.pallas_call(functools.partial(kernel, sizes), out_shape=(jax.ShapeDtyp...  42.6 us
    pallas_call x1, Pallas kernels, written(): pl.pallas_call(writer, out_shape=tuple((jax.ShapeDtypeStruct(v.shape, v.d...  1 us

profile of v5, /device:TPU:1, one launch (start us, length us, event | category | flops | bytes accessed | tf_op | source)
XLA Modules:
  0.0 44.3 jit_solution(2963354462523635043)
XLA Ops:
  0.6 42.6 %shard_map.67 = (bf16[16,128,128]{2,1,0:T(8,128)(2,1)S(1)}, bf16[16,128,128]{2,1,0:T(8,128)(2,1)S(1)}, f32[1,2]{1,0:T(1,128)S(1)}) custom-call(s32[1,16]{1,0:T(1,128)} %bitcast.1, s32[1,16]{1,0:T(1,128)} %pool_hbm.1, bf16[16,128,128]{2,1,0:T(8,128)(2,1)} %g_hbm.1, bf16[16,128,128]{2,1,0:T(8,128)(2,1)} %m_hbm.1), custom_call_target="tpu_custom_call" | custom-call | tf_op jit(solution)/shard_map/pallas_call | solution.py:461
  43.3 1.0 %shard_map.68 = (bf16[16,128,128]{2,1,0:T(8,128)(2,1)}, bf16[16,128,128]{2,1,0:T(8,128)(2,1)}, f32[1,2]{1,0:T(1,128)}) custom-call(bf16[16,128,128]{2,1,0:T(8,128)(2,1)S(1)} %get-tuple-element.6.refs_0_, bf16[16,128,128]{2,1,0:T(8,128)(2,1)S(1)} %get-tuple-element.7.refs_1_, f32[1,2]{1,0:T(1,128)S(1)} %get-tuple-element.8.refs_2_), custom_call_target="tpu_custom_call" | custom-call | tf_op jit(solution)/shard_map/pallas_call | solution.py:403

commit v6 on v5

--- a/solution.py
+++ b/solution.py
@@ -199,6 +199,14 @@
             at = jnp.where(codes[j] == q, j, at)
         return at
 
+    left, right, far = lax.rem(x + NX - 1, NX), lax.rem(x + 1, NX), lax.rem(x + 2, NX)
+    order = [far, left, right, x]
+    blocks = {}
+    for whose, core in (("theirs", 1 - c), ("ours", c)):
+        for i, at in enumerate(order):
+            p = lax.rem(2 * at + core + NZ - z, NZ)
+            blocks[whose, i] = (p, [source(2 * p), source(2 * p + 1)])
+
     for pair in loads:
         for cp in pair:
             cp.wait()
@@ -208,12 +216,32 @@
         velocity = momentum_rate * mbuf[j].astype(jnp.float32) + grad
         return velocity, (grad + momentum_rate * velocity).astype(jnp.bfloat16)
 
-    def make_pair(core, at):
-        p = lax.rem(2 * at + core + NZ - z, NZ)
+    def over_z(d):
+        to = lax.rem(z + d, NZ)
+        return remote(
+            yq.at[pl.ds(2 * to, 2)], yr.at[pl.ds(2 * z, 2)], z_send.at[d], z_recv.at[d], (f, to)
+        )
+
+    mine = pltpu.make_async_copy(yq.at[pl.ds(2 * z, 2)], yr.at[pl.ds(2 * z, 2)], z_recv.at[0])
+
+    def send_y(p):
+        d = lax.rem(p + NZ - z, NZ)
+
+        @pl.when(d != 0)
+        def _():
+            over_z(d).start()
+
+        @pl.when(d == 0)
+        def _():
+            mine.start()
+
+    def make_pair(whose, i):
+        core, at = (c if whose == "ours" else 1 - c), order[i]
+        p, taken = blocks[whose, i]
         grams = []
         for e in range(2):
             q = 2 * p + e
-            _, value = nesterov(source(q))
+            _, value = nesterov(taken[e])
             yq[q] = value
             wide = value.astype(jnp.float32)
             t0[pl.ds(q, 1), :] = jnp.sum(wide * wide, axis=0, keepdims=True)
@@ -229,24 +257,17 @@
         sent.append(copy)
         return copy
 
-    left, right, far = lax.rem(x + NX - 1, NX), lax.rem(x + 1, NX), lax.rem(x + 2, NX)
-    order = [far, left, right, x]
     cc = []
     for i, at in enumerate(order):
-        make_pair(1 - c, at)
+        make_pair("theirs", i)
         if i == 0:
             pl.semaphore_wait(barrier, (NZ - 1) + (NY - 1) + (NX - 1) + 1)
         cc.append(go(remote(pk.at[1 - c, at], r0.at[at], c_send.at[i], c_recv.at[i], partner)))
-    for at in order:
-        make_pair(c, at)
+        send_y(blocks["theirs", i][0])
+    for i in range(NX):
+        make_pair("ours", i)
+        send_y(blocks["ours", i][0])
     ct = go(remote(t0, t0r, c_send.at[NX], c_recv.at[NX], partner))
-
-    zc = []
-    for d in sorted(range(1, NZ), key=lambda d: -min(d, NZ - d)):
-        to = lax.rem(z + d, NZ)
-        zc.append(go(remote(yq.at[pl.ds(2 * to, 2)], yr.at[pl.ds(2 * z, 2)], z_send.at[d], z_recv.at[d], zdev(d))))
-    mine = pltpu.make_async_copy(yq.at[pl.ds(2 * z, 2)], yr.at[pl.ds(2 * z, 2)], z_recv.at[0])
-    mine.start()
 
     upper, lower = pl.ds(0, H // 2), pl.ds(H // 2, PACKED - H // 2)
     to_right = {"device": dev(y, right, c, z)}
@@ -348,8 +369,8 @@
         xa[d] = go(remote(qall.at[k], qall.at[k], a_send.at[d], a_recv.at[d], xdev(d)))
 
     mine.wait()
-    for cp in zc:
-        cp.wait_recv()
+    for d in range(1, NZ):
+        over_z(d).wait_recv()
     factor = step_size * 0.2 * math.sqrt(H * NK * NY)
 
     def apply(at):
@@ -383,6 +404,8 @@
 
     for cp in sent:
         cp.wait_send()
+    for d in range(1, NZ):
+        over_z(d).wait_send()
 
     @pl.when(plane != z)
     def _():

time: 44.4 us -> 44.1 us (level)
  no operation moved by 1% of the time
where the time goes in v6:
time: 44.1 us; the launch traced here: 43.9 us
  Pallas kernels  43.3 us (98%)
  between operations  0.64 us (1%)
    pallas_call x1, Pallas kernels, local(): pl.pallas_call(functools.partial(kernel, sizes), out_shape=(jax.ShapeDtyp...  42.3 us
    pallas_call x1, Pallas kernels, written(): pl.pallas_call(writer, out_shape=tuple((jax.ShapeDtypeStruct(v.shape, v.d...  1 us

profile of v6, /device:TPU:1, one launch (start us, length us, event | category | flops | bytes accessed | tf_op | source)
XLA Modules:
  0.0 43.9 jit_solution(9368865704637032370)
XLA Ops:
  0.6 42.3 %shard_map.67 = (bf16[16,128,128]{2,1,0:T(8,128)(2,1)S(1)}, bf16[16,128,128]{2,1,0:T(8,128)(2,1)S(1)}, f32[1,2]{1,0:T(1,128)S(1)}) custom-call(s32[1,16]{1,0:T(1,128)} %bitcast.1, s32[1,16]{1,0:T(1,128)} %pool_hbm.1, bf16[16,128,128]{2,1,0:T(8,128)(2,1)} %g_hbm.1, bf16[16,128,128]{2,1,0:T(8,128)(2,1)} %m_hbm.1), custom_call_target="tpu_custom_call" | custom-call | tf_op jit(solution)/shard_map/pallas_call | solution.py:484
  42.9 1.0 %shard_map.68 = (bf16[16,128,128]{2,1,0:T(8,128)(2,1)}, bf16[16,128,128]{2,1,0:T(8,128)(2,1)}, f32[1,2]{1,0:T(1,128)}) custom-call(bf16[16,128,128]{2,1,0:T(8,128)(2,1)S(1)} %get-tuple-element.6.refs_0_, bf16[16,128,128]{2,1,0:T(8,128)(2,1)S(1)} %get-tuple-element.7.refs_1_, f32[1,2]{1,0:T(1,128)S(1)} %get-tuple-element.8.refs_2_), custom_call_target="tpu_custom_call" | custom-call | tf_op jit(solution)/shard_map/pallas_call | solution.py:426

commit v7 on v6

--- a/solution.py
+++ b/solution.py
@@ -363,10 +363,10 @@
     a, b = newton_schulz(list(get_packed(gram)))
     put_packed(qall.at[k], a, b)
 
-    b_own = go(remote(qall.at[k], qall.at[k], b_send.at[0], b_recv.at[0], partner))
     xa = {}
     for d in (2, 1, 3):
         xa[d] = go(remote(qall.at[k], qall.at[k], a_send.at[d], a_recv.at[d], xdev(d)))
+    b_own = go(remote(qall.at[k], qall.at[k], b_send.at[0], b_recv.at[0], partner))
 
     mine.wait()
     for d in range(1, NZ):

time: 44.1 us -> 44.1 us (level)
  no operation moved by 1% of the time
where the time goes in v7:
time: 44.1 us; the launch traced here: 43.9 us
  Pallas kernels  43.3 us (98%)
  between operations  0.64 us (1%)
    pallas_call x1, Pallas kernels, local(): pl.pallas_call(functools.partial(kernel, sizes), out_shape=(jax.ShapeDtyp...  42.3 us
    pallas_call x1, Pallas kernels, written(): pl.pallas_call(writer, out_shape=tuple((jax.ShapeDtypeStruct(v.shape, v.d...  1 us

profile of v7, /device:TPU:1, one launch (start us, length us, event | category | flops | bytes accessed | tf_op | source)
XLA Modules:
  0.0 43.9 jit_solution(16277244665230389820)
XLA Ops:
  0.6 42.3 %shard_map.67 = (bf16[16,128,128]{2,1,0:T(8,128)(2,1)S(1)}, bf16[16,128,128]{2,1,0:T(8,128)(2,1)S(1)}, f32[1,2]{1,0:T(1,128)S(1)}) custom-call(s32[1,16]{1,0:T(1,128)} %bitcast.1, s32[1,16]{1,0:T(1,128)} %pool_hbm.1, bf16[16,128,128]{2,1,0:T(8,128)(2,1)} %g_hbm.1, bf16[16,128,128]{2,1,0:T(8,128)(2,1)} %m_hbm.1), custom_call_target="tpu_custom_call" | custom-call | tf_op jit(solution)/shard_map/pallas_call | solution.py:484
  42.9 1.0 %shard_map.68 = (bf16[16,128,128]{2,1,0:T(8,128)(2,1)}, bf16[16,128,128]{2,1,0:T(8,128)(2,1)}, f32[1,2]{1,0:T(1,128)}) custom-call(bf16[16,128,128]{2,1,0:T(8,128)(2,1)S(1)} %get-tuple-element.6.refs_0_, bf16[16,128,128]{2,1,0:T(8,128)(2,1)S(1)} %get-tuple-element.7.refs_1_, f32[1,2]{1,0:T(1,128)S(1)} %get-tuple-element.8.refs_2_), custom_call_target="tpu_custom_call" | custom-call | tf_op jit(solution)/shard_map/pallas_call | solution.py:426
